TPU v7x, 32 devices: a whole 2x2x4 slice. The times are simulated.
32 devices in a mesh: gx: 4 (over y, core), gy: 8 (over z, x).
Axes of the slice: x: 2, y: 2, z: 4, core: 2. Of those that a mesh axis runs over, the one named last changes fastest.
Arguments:
- conserved: float32 [5, 16, 128, 128], P(None, 'gx', 'gy'), as said below
Outputs:
- increment: float32 [5, 16, 128, 128], P(None, 'gx', 'gy')
- blending: float32 [4, 32, 32], P('gx', 'gy')
Inputs may be any that keep to these rules, and one draw needn't show every extreme that they name: `conserved`: every node's density and pressure are positive.
All inputs are finite; a program needn't handle non-finite values. Where the computation divides by a largest or mean magnitude, that divisor is 1e-20 or more.
Results may differ from a plain program's by a relative error of at most 0.0003.
Values sent between devices are 32-bit elements; how exact they have to be, the bound alone decides.
A program may use at most 64 MiB of HBM per device.

v0:
```python
import math

import jax
import jax.numpy as jnp
import numpy as np
from jax import lax
from jax.experimental import pallas as pl
from jax.experimental.pallas import tpu as pltpu
from jax.sharding import PartitionSpec as P

gas_gamma = 1.4
MESH = pl.DeviceIdType.MESH
BASE = 8
VEL, PRS, SND, LND, LNR, RAT = 5, 8, 9, 10, 11, 12
FIELDS = 13


def tables():
    inverse_root = 1.0 / math.sqrt(5.0)
    points = np.array([-1.0, -inverse_root, inverse_root, 1.0])
    weights = [1.0 / 6.0, 5.0 / 6.0, 5.0 / 6.0, 1.0 / 6.0]
    barycentric = np.array(
        [
            1.0 / np.prod([points[target] - points[other] for other in range(4) if other != target])
            for target in range(4)
        ]
    )
    derivative = np.zeros((4, 4))
    for target in range(4):
        for source in range(4):
            if target != source:
                derivative[target, source] = (
                    barycentric[source] / barycentric[target] / (points[target] - points[source])
                )
    legendre = np.stack(
        [np.ones(4), points, (3.0 * points**2 - 1.0) / 2.0, (5.0 * points**3 - 3.0 * points) / 2.0],
        1,
    )
    legendre = legendre * np.sqrt(np.arange(4) + 0.5)
    weight_column = np.array(weights)[:, None]
    discrete_norms = np.sum(weight_column * legendre * legendre, 0)
    inverse = (weight_column * legendre).T / discrete_norms[:, None]
    return (weights, derivative, inverse)


def primitives(conserved):
    density, m1, m2, m3, energy = conserved
    v1, v2, v3 = m1 / density, m2 / density, m3 / density
    pressure = (gas_gamma - 1.0) * (energy - 0.5 * density * (v1 * v1 + v2 * v2 + v3 * v3))
    ratio = density / pressure
    sound = jnp.sqrt(gas_gamma * pressure / density)
    return [density, m1, m2, m3, energy, v1, v2, v3, pressure, sound,
            jnp.log(density), jnp.log(ratio), ratio]


def mean_parts(a, b, log_a, log_b):
    total, gap = a + b, a - b
    relative = gap / total
    square = relative * relative
    small = square < 0.01
    series = 2.0 + square * (2.0 / 3.0 + square * (2.0 / 5.0 + square * (2.0 / 7.0)))
    return jnp.where(small, total, gap), jnp.where(small, series, log_a - log_b)


def entropy_flux(a, b, normal):
    num, den = mean_parts(a[0], b[0], a[LND], b[LND])
    mean_density = num / den
    num, den = mean_parts(a[RAT], b[RAT], a[LNR], b[LNR])
    inverse_beta = den / num
    velocity = [0.5 * (a[VEL + i] + b[VEL + i]) for i in range(3)]
    pressure = 0.5 * (a[PRS] + b[PRS])
    product = 0.5 * (a[5] * b[5] + a[6] * b[6] + a[7] * b[7])
    mass = mean_density * velocity[normal]
    out = [mass]
    for other in range(3):
        momentum = mass * velocity[other]
        out.append(momentum + pressure if other == normal else momentum)
    out.append(
        mass * (product + inverse_beta * (1.0 / (gas_gamma - 1.0)))
        + 0.5 * (a[PRS] * b[VEL + normal] + b[PRS] * a[VEL + normal])
    )
    return out


def dissipated(flux, a, b, normal):
    half = 0.5 * jnp.maximum(
        jnp.abs(a[VEL + normal]) + a[SND], jnp.abs(b[VEL + normal]) + b[SND]
    )
    return [flux[i] - half * (b[i] - a[i]) for i in range(5)]


def line_terms(nodes, normal, weights, deriv):
    vol = [[0.0] * 5 for _ in range(4)]
    diff = [[0.0] * 5 for _ in range(4)]
    for i in range(4):
        for j in range(i + 1, 4):
            flux = entropy_flux(nodes[i], nodes[j], normal)
            ci, cj = 2.0 * float(deriv[i, j]), 2.0 * float(deriv[j, i])
            if j == i + 1:
                face = dissipated(flux, nodes[i], nodes[j], normal)
            for f in range(5):
                vi, vj = ci * flux[f], cj * flux[f]
                vol[i][f] = vol[i][f] + vi
                vol[j][f] = vol[j][f] + vj
                if j == i + 1:
                    diff[i][f] = diff[i][f] + (face[f] * (1.0 / weights[i]) - vi)
                    diff[j][f] = diff[j][f] - (face[f] * (1.0 / weights[j]) + vj)
                else:
                    diff[i][f] = diff[i][f] - vi
                    diff[j][f] = diff[j][f] - vj
    return vol, diff


def make_kernel(ngx, ngy, nx, ny, nz):
    weights, deriv, inverse = tables()
    exl, eyl, rows = nx // 4, ny // 4, nx * ny
    direct = ngx * ngy <= 64
    spread_of = lambda d, n: min(d, n - d)
    far_first = lambda o: -spread_of(o[0], ngx) - spread_of(o[1], ngy)
    along_x = [(d, 0) for d in range(1, ngx)]
    along_y = [(0, d) for d in range(1, ngy)]
    both = sorted([(i, j) for i in range(ngx) for j in range(ngy) if i or j], key=far_first)
    first, second = (both, []) if direct else (along_x, along_y)
    peers = both if direct else along_y + along_x
    group = 8 if (nx * eyl) % 8 == 0 else 4

    def kernel(u_in, inc, smooth_out, top_out, u, st, vol, dif, tq, ysend, yrecv, xrecv, yexp, rb, rbr, yb, bsc,
               mx, mx2, mxr, myr, xs, xr, ys, yr, bs, br, ms, mr, ns, nr, us):
        ix, iy = lax.axis_index("gx"), lax.axis_index("gy")
        load = pltpu.make_async_copy(u_in, u, us)
        load.start()
        barrier = pltpu.get_barrier_semaphore()
        def at_offset(o):
            return {"gx": lax.rem(ix + o[0], ngx), "gy": lax.rem(iy + o[1], ngy)}

        for o in peers:
            pl.semaphore_signal(barrier, 1, device_id=at_offset(o), device_id_type=MESH)
        xup, xdn = {"gx": lax.rem(ix + 1, ngx)}, {"gx": lax.rem(ix + ngx - 1, ngx)}
        yup, ydn = {"gy": lax.rem(iy + 1, ngy)}, {"gy": lax.rem(iy + ngy - 1, ngy)}

        def remote(src, dst, ss, rs, dev):
            return pltpu.make_async_remote_copy(
                src_ref=src, dst_ref=dst, send_sem=ss, recv_sem=rs, device_id=dev,
                device_id_type=MESH)

        load.wait()
        for f in range(5):
            ysend[0, f] = u[f, pl.ds(ny - 1, nx, ny), :]
            ysend[1, f] = u[f, pl.ds(0, nx, ny), :]

        lane = lax.broadcasted_iota(jnp.int32, (8, nz), 1)
        k = lane % 4
        k0, k1, k2, k3 = k == 0, k == 1, k == 2, k == 3

        def lanes(values):
            a, b, c, d = (float(v) for v in values)
            return jnp.where(k0, a, jnp.where(k1, b, jnp.where(k2, c, d))).astype(jnp.float32)

        def roll(x, s):
            return pltpu.roll(x, s % nz, 1)

        zcoef = {s: lanes([inverse[c, c + s] if 0 <= c + s < 4 else 0.0 for c in range(4)])
                 for s in range(-3, 4)}
        top = None
        for r in range(0, rows, 8):
            p = primitives([u[f, r:r + 8, :] for f in range(5)])
            for f in range(FIELDS):
                st[f, BASE + r:BASE + r + 8, :] = p[f]
            speed = jnp.abs(p[5]) + jnp.abs(p[6]) + jnp.abs(p[7]) + 3.0 * p[SND]
            top = speed if top is None else jnp.maximum(top, speed)
            q = p[0] * p[PRS]
            t = zcoef[0] * q
            for s in (-3, -2, -1, 1, 2, 3):
                t = t + zcoef[s] * roll(q, -s)
            tq[r:r + 8, :] = t
        mx[...] = jnp.max(top, axis=0, keepdims=True)

        pl.semaphore_wait(barrier, len(peers))
        copies = [
            remote(u.at[:, rows - ny:rows], xrecv.at[0], xs, xr, xup),
            remote(u.at[:, 0:ny], xrecv.at[1], xs, xr, xdn),
            remote(ysend.at[0], yrecv.at[0], ys, yr, yup),
            remote(ysend.at[1], yrecv.at[1], ys, yr, ydn),
        ]
        all_x = remote(xrecv, xrecv, xs, xr, xup)
        all_y = remote(yrecv, yrecv, ys, yr, yup)
        all_blends = remote(rbr, rbr, bs, br, xup)
        all_first = remote(mxr, mxr, ms, mr, at_offset(first[0]))
        if second:
            all_second = remote(myr, myr, ns, nr, at_offset(second[0]))
        maxes = [remote(mx, mxr.at[i], ms, mr, at_offset(o))
                 for i, o in enumerate(first)]
        for c in copies + maxes:
            c.start()

        ke = k[:eyl]
        for e in range(exl):
            nodes = [[tq[pl.ds((4 * e + i) * ny + j, eyl, 4), :] for j in range(4)]
                     for i in range(4)]
            half = [[sum(float(inverse[a, i]) * nodes[i][j] for i in range(4))
                     for j in range(4)] for a in range(4)]
            e2 = e3 = e4 = 0.0
            for a in range(4):
                for b in range(4):
                    m = sum(float(inverse[b, j]) * half[a][j] for j in range(4))
                    m = m * m
                    e4 = e4 + m
                    if a < 3 and b < 3:
                        e3 = e3 + m
                    if a < 2 and b < 2:
                        e2 = e2 + m
            e3 = jnp.where(ke < 3, e3, 0.0)
            e2 = jnp.where(ke < 2, e2, 0.0)

            def spread(x):
                x = x + jnp.where(ke % 2 == 0, roll(x, -1), roll(x, 1))
                return x + jnp.where(ke < 2, roll(x, -2), roll(x, 2))

            e2, e3, e4 = spread(e2), spread(e3), spread(e4)
            energy = jnp.maximum((e4 - e3) / (e4 + 1e-06), (e3 - e2) / (e3 + 1e-06))
            threshold = 0.5 * 10.0 ** (-1.8 * 4.0**0.25)
            sharp = math.log(9999.0) / threshold
            raw = 1.0 / (1.0 + jnp.exp(-sharp * (energy - threshold)))
            raw = jnp.minimum(raw, 0.5)
            rb[e] = raw
            yb[e, 8:8 + eyl, :] = raw
        blends = [
            remote(rb, rbr.at[0], bs, br, xup),
            remote(rb, rbr.at[1], bs, br, xdn),
            remote(rb, rbr.at[2], bs, br, yup),
            remote(rb, rbr.at[3], bs, br, ydn),
        ]
        for c in blends:
            c.start()

        ca = lanes([2 * deriv[0, 1], 2 * deriv[1, 2], 2 * deriv[2, 3], 1 / weights[3]])
        cb = lanes([2 * deriv[1, 0], 2 * deriv[2, 1], 2 * deriv[3, 2], -1 / weights[0]])
        da = lanes([1 / weights[0], 1 / weights[1], 1 / weights[2], 0.0])
        db = lanes([-1 / weights[1], -1 / weights[2], -1 / weights[3], 0.0])
        cam = jnp.where(k3, 0.0, ca)
        cbm = jnp.where(k3, 0.0, cb)
        mc = lanes([2 * deriv[0, 2], 2 * deriv[1, 3], 0.0, 2 * deriv[3, 0]])
        mr_ = lanes([2 * deriv[0, 3], 0.0, 2 * deriv[2, 0], 2 * deriv[3, 1]])

        def z_group(g, carry):
            row = pl.multiple_of(g * 8, 8)
            own = [st[f, pl.ds(row + BASE, 8), :] for f in range(FIELDS)]
            nxt = [roll(x, -1) for x in own]
            far = [None] * FIELDS
            for f in (0, 5, 6, 7, PRS, LND, LNR, RAT):
                far[f] = jnp.where(k < 2, roll(own[f], -2), roll(own[f], 3))
            f1 = entropy_flux(own, nxt, 2)
            g1 = dissipated(f1, own, nxt, 2)
            fm = entropy_flux(own, far, 2)
            for f in range(5):
                sel = jnp.where(k3, g1[f], f1[f])
                mm = mc * fm[f] + mr_ * jnp.where(k0, roll(fm[f], -3), roll(fm[f], 2))
                vol[f, pl.ds(row, 8), :] = ca * sel + roll(cb * sel, 1) + mm
                dif[f, pl.ds(row, 8), :] = (
                    (da * g1[f] - cam * f1[f]) + roll(db * g1[f] - cbm * f1[f], 1) - mm)
            return carry

        lax.fori_loop(0, rows // 8, z_group, 0)

        for e in range(exl):
            for h in range(0, ny, 8):
                at = [(4 * e + i) * ny + h for i in range(4)]
                nodes = [[st[f, BASE + r:BASE + r + 8, :] for f in range(FIELDS)] for r in at]
                va, da_ = line_terms(nodes, 0, weights, deriv)
                for i in range(4):
                    for f in range(5):
                        vol[f, at[i]:at[i] + 8, :] += va[i][f]
                        dif[f, at[i]:at[i] + 8, :] += da_[i][f]
        for g in range(0, nx * eyl, group):
            def rows_of(ref, f, i, base):
                return ref[f, pl.ds(base + 4 * g + i, group, 4), :]

            nodes = [[rows_of(st, f, i, BASE) for f in range(FIELDS)] for i in range(4)]
            va, da_ = line_terms(nodes, 1, weights, deriv)
            for i in range(4):
                for f in range(5):
                    vol[f, pl.ds(4 * g + i, group, 4), :] += va[i][f]
                    dif[f, pl.ds(4 * g + i, group, 4), :] += da_[i][f]

        def gathered():
            all_first.wait_recv()
            tops = [mx[...]] + [mxr[i] for i in range(len(first))]
            while len(tops) > 1:
                pairs = [jnp.maximum(a, b) for a, b in zip(tops[::2], tops[1::2])]
                tops = pairs + tops[2 * len(pairs):]
            return tops[0]

        maxes2 = []
        if second:
            mx2[...] = gathered()
            maxes2 = [remote(mx2, myr.at[i], ns, nr, at_offset(o))
                      for i, o in enumerate(second)]
        for c in maxes2:
            c.start()

        all_x.wait_recv()
        all_y.wait_recv()

        for h in range(0, ny, 8):
            for e in range(exl + 1):
                def side(slab):
                    if slab < 0:
                        return primitives([xrecv[0, f, h:h + 8, :] for f in range(5)])
                    if slab >= nx:
                        return primitives([xrecv[1, f, h:h + 8, :] for f in range(5)])
                    r = BASE + slab * ny + h
                    return [st[f, r:r + 8, :] for f in range(FIELDS)]

                a, b = side(4 * e - 1), side(4 * e)
                face = dissipated(entropy_flux(a, b, 0), a, b, 0)
                for f in range(5):
                    if e > 0:
                        r = (4 * e - 1) * ny + h
                        vol[f, r:r + 8, :] += face[f] * (1.0 / weights[3])
                    if e < exl:
                        r = 4 * e * ny + h
                        vol[f, r:r + 8, :] -= face[f] * (1.0 / weights[0])

        for s in range(2):
            p = primitives([yrecv[s, f] for f in range(5)])
            for f in range(FIELDS):
                yexp[s, f, pl.ds(0 if s == 0 else eyl - 1, nx, eyl), :] = p[f]
        for g in range(0, nx * eyl, group):
            ye = (lax.broadcasted_iota(jnp.int32, (group, nz), 0) + g) % eyl
            low, high = ye == 0, ye == eyl - 1
            n0 = [st[f, pl.ds(BASE + 4 * g, group, 4), :] for f in range(FIELDS)]
            n3 = [st[f, pl.ds(BASE + 4 * g + 3, group, 4), :] for f in range(FIELDS)]
            lo = [jnp.where(low, yexp[0, f, g:g + group, :],
                            st[f, pl.ds(BASE + 4 * g - 1, group, 4), :]) for f in range(FIELDS)]
            hi = [jnp.where(high, yexp[1, f, g:g + group, :],
                            st[f, pl.ds(BASE + 4 * g + 4, group, 4), :]) for f in range(FIELDS)]
            glo = dissipated(entropy_flux(lo, n0, 1), lo, n0, 1)
            ghi = dissipated(entropy_flux(n3, hi, 1), n3, hi, 1)
            for f in range(5):
                vol[f, pl.ds(4 * g, group, 4), :] -= glo[f] * (1.0 / weights[0])
                vol[f, pl.ds(4 * g + 3, group, 4), :] += ghi[f] * (1.0 / weights[3])

        all_blends.wait_recv()
        pick = (lax.broadcasted_iota(jnp.int32, (nz, nz // 4), 0)
                == 4 * lax.broadcasted_iota(jnp.int32, (nz, nz // 4), 1)).astype(jnp.float32)
        for e in range(exl):
            yb[e, 7:8, :] = rbr[2, e, eyl - 1:eyl, :]
            yb[e, 8 + eyl:9 + eyl, :] = rbr[3, e, 0:1, :]
            raw = rb[e]
            near = jnp.maximum(rbr[0, exl - 1] if e == 0 else rb[e - 1],
                               rbr[1, 0] if e == exl - 1 else rb[e + 1])
            near = jnp.maximum(near, jnp.maximum(yb[e, 7:7 + eyl, :], yb[e, 9:9 + eyl, :]))
            near = jnp.maximum(near, jnp.maximum(roll(raw, 4), roll(raw, -4)))
            smooth = jnp.maximum(raw, 0.5 * near)
            bsc[e] = smooth
            smooth_out[e] = jnp.dot(smooth, pick, precision=lax.Precision.HIGHEST,
                                    preferred_element_type=jnp.float32)

        lower = lax.broadcasted_iota(jnp.int32, (8, nz), 0) < 4
        for e in range(exl):
            for h in range(0, ny, 8):
                y = h // 4
                b = jnp.where(lower, bsc[e, y:y + 1, :], bsc[e, y + 1:y + 2, :])
                for i in range(4):
                    r = (4 * e + i) * ny + h
                    for f in range(5):
                        inc[f, r:r + 8, :] = vol[f, r:r + 8, :] + b * dif[f, r:r + 8, :]
        for c in (all_x, all_y, all_blends):
            c.wait_send()
        all_first.wait_send()
        if second:
            all_second.wait_recv()
            all_second.wait_send()
        top = mx2[...] if second else gathered()
        for i in range(len(second)):
            top = jnp.maximum(top, myr[i])
        top_out[...] = top

    f32 = jnp.float32
    dma = pltpu.SemaphoreType.DMA
    pad = BASE + rows + 8
    scratch = [
        pltpu.VMEM((5, rows, nz), f32),
        pltpu.VMEM((FIELDS, pad, nz), f32),
        pltpu.VMEM((5, rows, nz), f32),
        pltpu.VMEM((5, rows, nz), f32),
        pltpu.VMEM((rows, nz), f32),
        pltpu.VMEM((2, 5, nx, nz), f32),
        pltpu.VMEM((2, 5, nx, nz), f32),
        pltpu.VMEM((2, 5, ny, nz), f32),
        pltpu.VMEM((2, FIELDS, nx * eyl, nz), f32),
        pltpu.VMEM((exl, eyl, nz), f32),
        pltpu.VMEM((4, exl, eyl, nz), f32),
        pltpu.VMEM((exl, eyl + 16, nz), f32),
        pltpu.VMEM((exl, eyl, nz), f32),
        pltpu.VMEM((1, nz), f32),
        pltpu.VMEM((1, nz), f32),
        pltpu.VMEM((len(first), 1, nz), f32),
        pltpu.VMEM((max(len(second), 1), 1, nz), f32),
        dma, dma, dma, dma, dma, dma,
        dma, dma, dma, dma, dma,
    ]
    return kernel, scratch


def finish(raw, smooth, top, inc, bl):
    step = -0.25 / jnp.max(top[...], axis=(0, 1), keepdims=True)
    for f in range(5):
        inc[f] = step * raw[f]
    bl[...] = smooth[...]


def solution(mesh):
    ngx, ngy = mesh.shape["gx"], mesh.shape["gy"]

    def body(conserved):
        _, nx, ny, nz = conserved.shape
        kernel, scratch = make_kernel(ngx, ngy, nx, ny, nz)
        vmem = pl.BlockSpec(memory_space=pltpu.VMEM)
        shape = lambda *dims: jax.ShapeDtypeStruct(dims, jnp.float32)
        raw, smooth, top = pl.pallas_call(
            kernel,
            out_shape=(shape(5, nx * ny, nz), shape(nx // 4, ny // 4, nz // 4), shape(1, nz)),
            in_specs=[pl.BlockSpec(memory_space=pltpu.HBM)],
            out_specs=(vmem, vmem, vmem),
            scratch_shapes=scratch,
            compiler_params=pltpu.CompilerParams(
                collective_id=0, has_side_effects=True, vmem_limit_bytes=12 * 2**20),
            name="section",
        )(pltpu.with_memory_space_constraint(
            conserved.reshape(5, nx * ny, nz), pltpu.HBM))
        inc, blending = pl.pallas_call(
            finish,
            out_shape=(shape(5, nx * ny, nz), shape(nx // 4, ny // 4, nz // 4)),
            in_specs=[vmem, vmem, vmem],
            out_specs=(vmem, vmem),
            compiler_params=pltpu.CompilerParams(vmem_limit_bytes=8 * 2**20),
            name="finish",
        )(raw, smooth, top)
        return inc.reshape(conserved.shape), blending

    return jax.shard_map(
        body, mesh=mesh, in_specs=(P(None, "gx", "gy", None),),
        out_specs=(P(None, "gx", "gy", None), P("gx", "gy", None)), check_vma=False)
```

profile of v0, /device:TPU:0, one launch (start us, length us, event | category | flops | bytes accessed | tf_op | source)
XLA Modules:
  0.0 11.4 jit_solution(13569518381973282549)
XLA Ops:
  0.6 10.0 %section.1 = (f32[5,64,128]{2,1,0:T(8,128)S(1)}, f32[1,4,32]{2,1,0:T(4,128)S(1)}, f32[1,128]{1,0:T(1,128)S(1)}) custom-call(f32[5,64,128]{2,1,0:T(8,128)} %bitcast.2), custom_call_target="tpu_custom_call" | custom-call | tf_op jit(solution)/shard_map/section/pallas_call | solution.py:421
  10.6 0.8 %finish.1 = (f32[5,64,128]{2,1,0:T(8,128)}, f32[1,4,32]{2,1,0:T(4,128)}) custom-call(f32[5,64,128]{2,1,0:T(8,128)S(1)} %get-tuple-element.7.raw, f32[1,4,32]{2,1,0:T(4,128)S(1)} %get-tuple-element.8.smooth, f32[1,128]{1,0:T(1,128)S(1)} %get-tuple-element.9.top), custom_call_target="tpu_custom_call" | custom-call | tf_op jit(solution)/shard_map/finish/pallas_call | solution.py:432
where the time goes:
time: 11.6 us; the launch traced here: 11.4 us
  Pallas kernels  10.8 us (93%)
  between operations  0.64 us (6%)
    pallas_call x1, Pallas kernels, body(): pl.pallas_call(kernel, out_shape=(shape(5, nx * ny, nz), shape(nx // 4, n...  10 us
    pallas_call x1, Pallas kernels, body(): pl.pallas_call(finish, out_shape=(shape(5, nx * ny, nz), shape(nx // 4, n...  0.8 us

commit v1 on v0

v1 whole, which is shorter than its diff:
```python
import math

import jax
import jax.numpy as jnp
import numpy as np
from jax import lax
from jax.experimental import pallas as pl
from jax.experimental.pallas import tpu as pltpu
from jax.sharding import PartitionSpec as P

gas_gamma = 1.4
MESH = pl.DeviceIdType.MESH
BASE = 8
VEL, PRS, SND, LND, LNR, RAT = 5, 8, 9, 10, 11, 12
FIELDS = 13


def tables():
    inverse_root = 1.0 / math.sqrt(5.0)
    points = np.array([-1.0, -inverse_root, inverse_root, 1.0])
    weights = [1.0 / 6.0, 5.0 / 6.0, 5.0 / 6.0, 1.0 / 6.0]
    barycentric = np.array(
        [
            1.0 / np.prod([points[target] - points[other] for other in range(4) if other != target])
            for target in range(4)
        ]
    )
    derivative = np.zeros((4, 4))
    for target in range(4):
        for source in range(4):
            if target != source:
                derivative[target, source] = (
                    barycentric[source] / barycentric[target] / (points[target] - points[source])
                )
    legendre = np.stack(
        [np.ones(4), points, (3.0 * points**2 - 1.0) / 2.0, (5.0 * points**3 - 3.0 * points) / 2.0],
        1,
    )
    legendre = legendre * np.sqrt(np.arange(4) + 0.5)
    weight_column = np.array(weights)[:, None]
    discrete_norms = np.sum(weight_column * legendre * legendre, 0)
    inverse = (weight_column * legendre).T / discrete_norms[:, None]
    return (weights, derivative, inverse)


def mechanics(conserved):
    density, m1, m2, m3, energy = conserved
    inverse = 1.0 / density
    v1, v2, v3 = m1 * inverse, m2 * inverse, m3 * inverse
    pressure = (gas_gamma - 1.0) * (energy - 0.5 * density * (v1 * v1 + v2 * v2 + v3 * v3))
    sound = jnp.sqrt(gas_gamma * pressure * inverse)
    return [v1, v2, v3, pressure, sound]


def logarithms(density, pressure):
    ratio = density / pressure
    return [jnp.log(density), jnp.log(ratio), ratio]


def primitives(conserved):
    motion = mechanics(conserved)
    return list(conserved) + motion + logarithms(conserved[0], motion[3])


def mean_parts(a, b, log_a, log_b):
    total, gap = a + b, a - b
    relative = gap / total
    square = relative * relative
    small = square < 0.01
    series = 2.0 + square * (2.0 / 3.0 + square * (2.0 / 5.0 + square * (2.0 / 7.0)))
    return jnp.where(small, total, gap), jnp.where(small, series, log_a - log_b)


def entropy_flux(a, b, normal):
    num, den = mean_parts(a[0], b[0], a[LND], b[LND])
    mean_density = num / den
    num, den = mean_parts(a[RAT], b[RAT], a[LNR], b[LNR])
    inverse_beta = den / num
    velocity = [0.5 * (a[VEL + i] + b[VEL + i]) for i in range(3)]
    pressure = 0.5 * (a[PRS] + b[PRS])
    product = 0.5 * (a[5] * b[5] + a[6] * b[6] + a[7] * b[7])
    mass = mean_density * velocity[normal]
    out = [mass]
    for other in range(3):
        momentum = mass * velocity[other]
        out.append(momentum + pressure if other == normal else momentum)
    out.append(
        mass * (product + inverse_beta * (1.0 / (gas_gamma - 1.0)))
        + 0.5 * (a[PRS] * b[VEL + normal] + b[PRS] * a[VEL + normal])
    )
    return out


def dissipated(flux, a, b, normal):
    half = 0.5 * jnp.maximum(
        jnp.abs(a[VEL + normal]) + a[SND], jnp.abs(b[VEL + normal]) + b[SND]
    )
    return [flux[i] - half * (b[i] - a[i]) for i in range(5)]


def line_terms(nodes, normal, weights, deriv):
    vol = [[0.0] * 5 for _ in range(4)]
    diff = [[0.0] * 5 for _ in range(4)]
    for i in range(4):
        for j in range(i + 1, 4):
            flux = entropy_flux(nodes[i], nodes[j], normal)
            ci, cj = 2.0 * float(deriv[i, j]), 2.0 * float(deriv[j, i])
            if j == i + 1:
                face = dissipated(flux, nodes[i], nodes[j], normal)
            for f in range(5):
                vi, vj = ci * flux[f], cj * flux[f]
                vol[i][f] = vol[i][f] + vi
                vol[j][f] = vol[j][f] + vj
                if j == i + 1:
                    diff[i][f] = diff[i][f] + (face[f] * (1.0 / weights[i]) - vi)
                    diff[j][f] = diff[j][f] - (face[f] * (1.0 / weights[j]) + vj)
                else:
                    diff[i][f] = diff[i][f] - vi
                    diff[j][f] = diff[j][f] - vj
    return vol, diff


def make_kernel(ngx, ngy, nx, ny, nz):
    weights, deriv, inverse = tables()
    exl, eyl, rows = nx // 4, ny // 4, nx * ny
    total = ngx * ngy
    roots = [(0, 0), (1, 0), (ngx - 1, 0)]
    group = 8 if (nx * eyl) % 8 == 0 else 4

    def kernel(u_in, inc, smooth_out, top_out, st, vol, dif, tq, ysend, yrecv, xrecv, yown, rb, rbr, near,
               bsc, mx, mx2, mxr, myr, xs, xr, ys, yr, bs, br, ms, mr, ns, nr, us, late):
        ix, iy = lax.axis_index("gx"), lax.axis_index("gy")
        loads = [pltpu.make_async_copy(u_in.at[f], st.at[f, BASE:BASE + rows], us) for f in range(5)]
        for c in loads:
            c.start()
        barrier = pltpu.get_barrier_semaphore()
        rank = iy * ngx + ix
        is_root = [rank == y * ngx + x for x, y in roots]
        hub = is_root[-1]
        root = jnp.logical_or(jnp.logical_or(is_root[0], is_root[1]), hub)

        def greet(device):
            pl.semaphore_signal(barrier, 1, device_id=device, device_id_type=MESH)

        def visit(act):
            def step(k, carry):
                t = k + jnp.where(k >= rank, 1, 0)
                act({"gx": lax.rem(t, ngx), "gy": lax.div(t, ngx)})
                return carry

            lax.fori_loop(0, total - 1, step, 0)

        xup, xdn = {"gx": lax.rem(ix + 1, ngx)}, {"gx": lax.rem(ix + ngx - 1, ngx)}
        yup, ydn = {"gy": lax.rem(iy + 1, ngy)}, {"gy": lax.rem(iy + ngy - 1, ngy)}
        inner, wraps = iy > 0, iy == ngy - 1
        for device in (xup, xdn, ydn):
            greet(device)
        pl.when(jnp.logical_not(wraps))(lambda: greet(yup))

        @pl.when(root)
        def _():
            visit(greet)


        def remote(src, dst, ss, rs, dev):
            return pltpu.make_async_remote_copy(
                src_ref=src, dst_ref=dst, send_sem=ss, recv_sem=rs, device_id=dev,
                device_id_type=MESH)

        all_x = remote(xrecv, xrecv, xs, xr, xup)
        all_y = remote(yrecv, yrecv, ys, yr, yup)
        all_blends = remote(rbr, rbr, bs, br, xup)
        others = mxr.at[0:total - 1]
        all_tops = remote(others, others, ms, mr, xup)

        pltpu.make_async_copy(u_in, st.at[0:5, BASE:BASE + rows], us).wait()
        top = None
        for r in range(0, rows, 8):
            here = slice(BASE + r, BASE + r + 8)
            p = mechanics([st[f, here, :] for f in range(5)])
            for f in range(5):
                st[VEL + f, here, :] = p[f]
            speed = jnp.abs(p[0]) + jnp.abs(p[1]) + jnp.abs(p[2]) + 3.0 * p[4]
            top = speed if top is None else jnp.maximum(top, speed)
        mx[...] = jnp.max(top, axis=0, keepdims=True)
        for f in range(5):
            ysend[0, f] = st[f, pl.ds(BASE + ny - 1, nx, ny), :]
            ysend[1, f] = st[f, pl.ds(BASE, nx, ny), :]
        mxr[rank] = mx[...]

        pl.semaphore_wait(barrier, jnp.where(root, 5, 6) + jnp.where(inner, 1, 0))

        @pl.when(wraps)
        def _():
            pl.semaphore_signal(late, 1, device_id=yup, device_id_type=MESH)

        for (x, y), here in zip(roots, is_root):
            @pl.when(jnp.logical_not(here))
            def _():
                remote(mx, mxr.at[rank], ms, mr, {"gx": x, "gy": y}).start()

        remote(ysend.at[0], yrecv.at[0], ys, yr, yup).start()
        pl.when(inner)(lambda: remote(ysend.at[1], yrecv.at[1], ys, yr, ydn).start())
        remote(st.at[0:5, BASE + rows - ny:BASE + rows], xrecv.at[0], xs, xr, xup).start()
        remote(st.at[0:5, BASE:BASE + ny], xrecv.at[1], xs, xr, xdn).start()

        lane = lax.broadcasted_iota(jnp.int32, (8, nz), 1)
        k = lane % 4
        k0, k1, k2, k3 = k == 0, k == 1, k == 2, k == 3

        def lanes(values):
            a, b, c, d = (float(v) for v in values)
            return jnp.where(k0, a, jnp.where(k1, b, jnp.where(k2, c, d))).astype(jnp.float32)

        def roll(x, s):
            return pltpu.roll(x, s % nz, 1)

        zcoef = {s: lanes([inverse[c, c + s] if 0 <= c + s < 4 else 0.0 for c in range(4)])
                 for s in range(-3, 4)}
        for r in range(0, rows, 8):
            here = slice(BASE + r, BASE + r + 8)
            q = st[0, here, :] * st[PRS, here, :]
            t = zcoef[0] * q
            for s in (-3, -2, -1, 1, 2, 3):
                t = t + zcoef[s] * roll(q, -s)
            tq[r:r + 8, :] = t

        ke = k[:eyl]
        for e in range(exl):
            nodes = [[tq[pl.ds((4 * e + i) * ny + j, eyl, 4), :] for j in range(4)]
                     for i in range(4)]
            half = [[sum(float(inverse[a, i]) * nodes[i][j] for i in range(4))
                     for j in range(4)] for a in range(4)]
            e2 = e3 = e4 = 0.0
            for a in range(4):
                for b in range(4):
                    m = sum(float(inverse[b, j]) * half[a][j] for j in range(4))
                    m = m * m
                    e4 = e4 + m
                    if a < 3 and b < 3:
                        e3 = e3 + m
                    if a < 2 and b < 2:
                        e2 = e2 + m
            e3 = jnp.where(ke < 3, e3, 0.0)
            e2 = jnp.where(ke < 2, e2, 0.0)

            def spread(x):
                total = x
                for s in range(1, 4):
                    total = total + jnp.where(ke + s < 4, roll(x, -s), roll(x, 4 - s))
                return total

            e2, e3, e4 = spread(e2), spread(e3), spread(e4)
            energy = jnp.maximum((e4 - e3) / (e4 + 1e-06), (e3 - e2) / (e3 + 1e-06))
            threshold = 0.5 * 10.0 ** (-1.8 * 4.0**0.25)
            sharp = math.log(9999.0) / threshold
            raw = 1.0 / (1.0 + jnp.exp(-sharp * (energy - threshold)))
            raw = jnp.minimum(raw, 0.5)
            rb[e] = raw
        remote(rb, rbr.at[2], bs, br, yup).start()
        pl.when(inner)(lambda: remote(rb, rbr.at[3], bs, br, ydn).start())
        remote(rb, rbr.at[0], bs, br, xup).start()
        remote(rb, rbr.at[1], bs, br, xdn).start()

        for r in range(0, rows, 8):
            here = slice(BASE + r, BASE + r + 8)
            p = logarithms(st[0, here, :], st[PRS, here, :])
            for f in range(3):
                st[LND + f, here, :] = p[f]
        for e in range(exl):
            raw = rb[e]
            close = jnp.maximum(roll(raw, 4), roll(raw, -4))
            if e > 0:
                close = jnp.maximum(close, rb[e - 1])
            if e < exl - 1:
                close = jnp.maximum(close, rb[e + 1])
            near[e, 8:8 + eyl, :] = raw
            near[e, 7:8, :] = raw[0:1]
            near[e, 8 + eyl:9 + eyl, :] = raw[eyl - 1:eyl]
            close = jnp.maximum(close, jnp.maximum(near[e, 7:7 + eyl, :], near[e, 9:9 + eyl, :]))
            bsc[e] = close

        ca = lanes([2 * deriv[0, 1], 2 * deriv[1, 2], 2 * deriv[2, 3], 1 / weights[3]])
        cb = lanes([2 * deriv[1, 0], 2 * deriv[2, 1], 2 * deriv[3, 2], -1 / weights[0]])
        da = lanes([1 / weights[0], 1 / weights[1], 1 / weights[2], 0.0])
        db = lanes([-1 / weights[1], -1 / weights[2], -1 / weights[3], 0.0])
        cam = jnp.where(k3, 0.0, ca)
        cbm = jnp.where(k3, 0.0, cb)
        mc = lanes([2 * deriv[0, 2], 2 * deriv[1, 3], 0.0, 2 * deriv[3, 0]])
        mr_ = lanes([2 * deriv[0, 3], 0.0, 2 * deriv[2, 0], 2 * deriv[3, 1]])

        def z_group(g, carry):
            row = g * 8
            own = [st[f, pl.ds(row + BASE, 8), :] for f in range(FIELDS)]
            nxt = [roll(x, -1) for x in own]
            far = [None] * FIELDS
            for f in (0, 5, 6, 7, PRS, LND, LNR, RAT):
                far[f] = jnp.where(k < 2, roll(own[f], -2), roll(own[f], 3))
            f1 = entropy_flux(own, nxt, 2)
            g1 = dissipated(f1, own, nxt, 2)
            fm = entropy_flux(own, far, 2)
            for f in range(5):
                sel = jnp.where(k3, g1[f], f1[f])
                mm = mc * fm[f] + mr_ * jnp.where(k0, roll(fm[f], -3), roll(fm[f], 2))
                vol[f, pl.ds(row, 8), :] = ca * sel + roll(cb * sel, 1) + mm
                dif[f, pl.ds(row, 8), :] = (
                    (da * g1[f] - cam * f1[f]) + roll(db * g1[f] - cbm * f1[f], 1) - mm)
            return carry

        for g in range(rows // 8):
            z_group(g, 0)

        for e in range(exl):
            for h in range(0, ny, 8):
                slabs = [(4 * e + i) * ny + h for i in range(4)]
                nodes = [[st[f, BASE + r:BASE + r + 8, :] for f in range(FIELDS)] for r in slabs]
                va, da_ = line_terms(nodes, 0, weights, deriv)
                for i in range(4):
                    for f in range(5):
                        vol[f, slabs[i]:slabs[i] + 8, :] += va[i][f]
                        dif[f, slabs[i]:slabs[i] + 8, :] += da_[i][f]
        for g in range(0, nx * eyl, group):
            def rows_of(ref, f, i, base):
                return ref[f, pl.ds(base + 4 * g + i, group, 4), :]

            nodes = [[rows_of(st, f, i, BASE) for f in range(FIELDS)] for i in range(4)]
            va, da_ = line_terms(nodes, 1, weights, deriv)
            for i in range(4):
                for f in range(5):
                    vol[f, pl.ds(4 * g + i, group, 4), :] += va[i][f]
                    dif[f, pl.ds(4 * g + i, group, 4), :] += da_[i][f]

        for e in range(1, exl):
            for h in range(0, ny, 8):
                r = 4 * e * ny + h
                a = [st[f, BASE + r - ny:BASE + r - ny + 8, :] for f in range(FIELDS)]
                b = [st[f, BASE + r:BASE + r + 8, :] for f in range(FIELDS)]
                face = dissipated(entropy_flux(a, b, 0), a, b, 0)
                for f in range(5):
                    vol[f, r - ny:r - ny + 8, :] += face[f] * (1.0 / weights[3])
                    vol[f, r:r + 8, :] -= face[f] * (1.0 / weights[0])
        for g in range(0, nx * eyl, group):
            ye = (lax.broadcasted_iota(jnp.int32, (group, nz), 0) + g) % eyl
            inside = ye < eyl - 1
            a = [st[f, pl.ds(BASE + 4 * g + 3, group, 4), :] for f in range(FIELDS)]
            b = [st[f, pl.ds(BASE + 4 * g + 4, group, 4), :] for f in range(FIELDS)]
            face = dissipated(entropy_flux(a, b, 1), a, b, 1)
            for f in range(5):
                kept = jnp.where(inside, face[f], 0.0)
                vol[f, pl.ds(4 * g + 3, group, 4), :] += kept * (1.0 / weights[3])
                vol[f, pl.ds(4 * g + 4, group, 4), :] -= kept * (1.0 / weights[0])
        for f in range(FIELDS):
            yown[f, 0:nx] = st[f, pl.ds(BASE, nx, ny), :]
            yown[f, nx:2 * nx] = st[f, pl.ds(BASE + ny - 1, nx, ny), :]

        @pl.when(jnp.logical_not(inner))
        def _():
            pl.semaphore_wait(late, 1)
            remote(ysend.at[1], yrecv.at[1], ys, yr, ydn).start()
            remote(rb, rbr.at[3], bs, br, ydn).start()

        all_x.wait_recv()
        for h in range(0, ny, 8):
            for side in range(2):
                got = primitives([xrecv[side, f, h:h + 8, :] for f in range(5)])
                r = h if side == 0 else rows - ny + h
                own = [st[f, BASE + r:BASE + r + 8, :] for f in range(FIELDS)]
                a, b = (got, own) if side == 0 else (own, got)
                face = dissipated(entropy_flux(a, b, 0), a, b, 0)
                scale = -1.0 / weights[0] if side == 0 else 1.0 / weights[3]
                for f in range(5):
                    vol[f, r:r + 8, :] += face[f] * scale

        all_y.wait_recv()
        all_blends.wait_recv()
        row = lax.broadcasted_iota(jnp.int32, (eyl, nz), 0)
        pick = (lax.broadcasted_iota(jnp.int32, (nz, nz // 4), 0)
                == 4 * lax.broadcasted_iota(jnp.int32, (nz, nz // 4), 1)).astype(jnp.float32)
        for e in range(exl):
            close = bsc[e]
            if e == 0:
                close = jnp.maximum(close, rbr[0, exl - 1])
            if e == exl - 1:
                close = jnp.maximum(close, rbr[1, 0])
            close = jnp.maximum(close, jnp.where(row == 0, rbr[2, e, eyl - 1:eyl, :], 0.0))
            close = jnp.maximum(close, jnp.where(row == eyl - 1, rbr[3, e, 0:1, :], 0.0))
            smooth = jnp.maximum(rb[e], 0.5 * close)
            bsc[e] = smooth
            smooth_out[e] = jnp.dot(smooth, pick, precision=lax.Precision.HIGHEST,
                                    preferred_element_type=jnp.float32)

        got = primitives([jnp.concatenate([yrecv[0, f], yrecv[1, f]], axis=0) for f in range(5)])
        own = [yown[f] for f in range(FIELDS)]
        first = lax.broadcasted_iota(jnp.int32, (2 * nx, nz), 0) < nx
        a = [jnp.where(first, got[f], own[f]) for f in range(FIELDS)]
        b = [jnp.where(first, own[f], got[f]) for f in range(FIELDS)]
        face = dissipated(entropy_flux(a, b, 1), a, b, 1)
        for f in range(5):
            vol[f, pl.ds(0, nx, ny), :] -= face[f][:nx] * (1.0 / weights[0])
            vol[f, pl.ds(ny - 1, nx, ny), :] += face[f][nx:] * (1.0 / weights[3])
        under = lax.broadcasted_iota(jnp.int32, (8, nz), 0) < 4
        for e in range(exl):
            for h in range(0, ny, 8):
                y = h // 4
                b = jnp.where(under, bsc[e, y:y + 1, :], bsc[e, y + 1:y + 2, :])
                for i in range(4):
                    r = (4 * e + i) * ny + h
                    for f in range(5):
                        inc[f, r:r + 8, :] = vol[f, r:r + 8, :] + b * dif[f, r:r + 8, :]
        for c in (all_x, all_y, all_blends):
            c.wait_send()

        for here in is_root:
            @pl.when(jnp.logical_not(here))
            def _():
                remote(mx, mxr.at[rank], ms, mr, xup).wait_send()

        @pl.when(root)
        def _():
            all_tops.wait_recv()
            tops = [mxr[i] for i in range(total)]
            while len(tops) > 1:
                pairs = [jnp.maximum(a, b) for a, b in zip(tops[::2], tops[1::2])]
                tops = pairs + tops[2 * len(pairs):]
            top_out[...] = tops[0]

            @pl.when(hub)
            def _():
                mx2[...] = tops[0]

                def spread(x, y):
                    return remote(mx2, myr, ns, nr, {"gx": x, "gy": y})

                for y in range(min(ngy, 64 // ngx)):
                    for x in range(ngx):
                        if (x, y) not in roots:
                            spread(x, y).start()

                def send(t, carry):
                    spread(lax.rem(t, ngx), lax.div(t, ngx)).start()
                    return carry

                def sent(t, carry):
                    spread(0, 0).wait_send()
                    return carry

                if total > 64:
                    lax.fori_loop(64 // ngx * ngx, total, send, 0)
                lax.fori_loop(0, total - len(roots), sent, 0)

        @pl.when(jnp.logical_not(root))
        def _():
            remote(mx2, myr, ns, nr, xup).wait_recv()
            top_out[...] = myr[...]

    f32 = jnp.float32
    dma = pltpu.SemaphoreType.DMA
    pad = BASE + rows + 8
    scratch = [
        pltpu.VMEM((FIELDS, pad, nz), f32),
        pltpu.VMEM((5, rows + 8, nz), f32),
        pltpu.VMEM((5, rows, nz), f32),
        pltpu.VMEM((rows, nz), f32),
        pltpu.VMEM((2, 5, nx, nz), f32),
        pltpu.VMEM((2, 5, nx, nz), f32),
        pltpu.VMEM((2, 5, ny, nz), f32),
        pltpu.VMEM((FIELDS, 2 * nx, nz), f32),
        pltpu.VMEM((exl, eyl, nz), f32),
        pltpu.VMEM((4, exl, eyl, nz), f32),
        pltpu.VMEM((exl, eyl + 16, nz), f32),
        pltpu.VMEM((exl, eyl, nz), f32),
        pltpu.VMEM((1, nz), f32),
        pltpu.VMEM((1, nz), f32),
        pltpu.VMEM((total, 1, nz), f32),
        pltpu.VMEM((1, nz), f32),
        dma, dma, dma, dma, dma, dma,
        dma, dma, dma, dma, dma,
        pltpu.SemaphoreType.REGULAR,
    ]
    return kernel, scratch


def finish(raw, smooth, top, inc, bl):
    step = -0.25 / jnp.max(top[...], axis=(0, 1), keepdims=True)
    for f in range(5):
        inc[f] = step * raw[f]
    bl[...] = smooth[...]


def solution(mesh):
    ngx, ngy = mesh.shape["gx"], mesh.shape["gy"]

    def body(conserved):
        _, nx, ny, nz = conserved.shape
        kernel, scratch = make_kernel(ngx, ngy, nx, ny, nz)
        vmem = pl.BlockSpec(memory_space=pltpu.VMEM)
        shape = lambda *dims: jax.ShapeDtypeStruct(dims, jnp.float32)
        raw, smooth, top = pl.pallas_call(
            kernel,
            out_shape=(shape(5, nx * ny, nz), shape(nx // 4, ny // 4, nz // 4), shape(1, nz)),
            in_specs=[pl.BlockSpec(memory_space=pltpu.HBM)],
            out_specs=(vmem, vmem, vmem),
            scratch_shapes=scratch,
            compiler_params=pltpu.CompilerParams(
                collective_id=0, has_side_effects=True, vmem_limit_bytes=12 * 2**20),
            name="section",
        )(pltpu.with_memory_space_constraint(
            conserved.reshape(5, nx * ny, nz), pltpu.HBM))
        inc, blending = pl.pallas_call(
            finish,
            out_shape=(shape(5, nx * ny, nz), shape(nx // 4, ny // 4, nz // 4)),
            in_specs=[vmem, vmem, vmem],
            out_specs=(vmem, vmem),
            compiler_params=pltpu.CompilerParams(vmem_limit_bytes=8 * 2**20),
            name="finish",
        )(raw, smooth, top)
        return inc.reshape(conserved.shape), blending

    return jax.shard_map(
        body, mesh=mesh, in_specs=(P(None, "gx", "gy", None),),
        out_specs=(P(None, "gx", "gy", None), P("gx", "gy", None)), check_vma=False)
```

time: 11.6 us -> 11.2 us (0.966)
  Pallas kernels: 10.8 us -> 10.3 us
    pallas_call x1, Pallas kernels: 10 us -> 9.53 us  [body(): pl.pallas_call(kernel, out_shape=(shape(5, nx * ny, nz), shape(nx // 4, n...]
where the time goes in v1:
time: 11.2 us; the launch traced here: 11 us
  Pallas kernels  10.3 us (92%)
  between operations  0.64 us (6%)
    pallas_call x1, Pallas kernels, body(): pl.pallas_call(kernel, out_shape=(shape(5, nx * ny, nz), shape(nx // 4, n...  9.53 us
    pallas_call x1, Pallas kernels, body(): pl.pallas_call(finish, out_shape=(shape(5, nx * ny, nz), shape(nx // 4, n...  0.8 us

profile of v1, /device:TPU:0, one launch (start us, length us, event | category | flops | bytes accessed | tf_op | source)
XLA Modules:
  0.0 11.0 jit_solution(8345391709834627237)
XLA Ops:
  0.6 9.5 %section.1 = (f32[5,64,128]{2,1,0:T(8,128)S(1)}, f32[1,4,32]{2,1,0:T(4,128)S(1)}, f32[1,128]{1,0:T(1,128)S(1)}) custom-call(f32[5,64,128]{2,1,0:T(8,128)} %bitcast.2), custom_call_target="tpu_custom_call" | custom-call | tf_op jit(solution)/shard_map/section/pallas_call | solution.py:498
  10.2 0.8 %finish.1 = (f32[5,64,128]{2,1,0:T(8,128)}, f32[1,4,32]{2,1,0:T(4,128)}) custom-call(f32[5,64,128]{2,1,0:T(8,128)S(1)} %get-tuple-element.7.raw, f32[1,4,32]{2,1,0:T(4,128)S(1)} %get-tuple-element.8.smooth, f32[1,128]{1,0:T(1,128)S(1)} %get-tuple-element.9.top), custom_call_target="tpu_custom_call" | custom-call | tf_op jit(solution)/shard_map/finish/pallas_call | solution.py:509

commit v2 on v1

--- a/solution.py
+++ b/solution.py
@@ -124,20 +124,21 @@
     weights, deriv, inverse = tables()
     exl, eyl, rows = nx // 4, ny // 4, nx * ny
     total = ngx * ngy
-    roots = [(0, 0), (1, 0), (ngx - 1, 0)]
+    parts = 10 * (nx + ny) + 4 * exl * eyl
+    roots = [(0, 0), (ngx - 1, 0), (1, 0)]
     group = 8 if (nx * eyl) % 8 == 0 else 4
 
     def kernel(u_in, inc, smooth_out, top_out, st, vol, dif, tq, ysend, yrecv, xrecv, yown, rb, rbr, near,
-               bsc, mx, mx2, mxr, myr, xs, xr, ys, yr, bs, br, ms, mr, ns, nr, us, late):
+               bsc, mx, mx2, mxr, myr, span, sent, halo, tops, late):
         ix, iy = lax.axis_index("gx"), lax.axis_index("gy")
-        loads = [pltpu.make_async_copy(u_in.at[f], st.at[f, BASE:BASE + rows], us) for f in range(5)]
+        loads = [pltpu.make_async_copy(u_in.at[f], st.at[f, BASE:BASE + rows], sent) for f in range(5)]
         for c in loads:
             c.start()
         barrier = pltpu.get_barrier_semaphore()
         rank = iy * ngx + ix
         is_root = [rank == y * ngx + x for x, y in roots]
-        hub = is_root[-1]
-        root = jnp.logical_or(jnp.logical_or(is_root[0], is_root[1]), hub)
+        hub = is_root[1]
+        root = jnp.logical_or(jnp.logical_or(is_root[0], is_root[2]), hub)
 
         def greet(device):
             pl.semaphore_signal(barrier, 1, device_id=device, device_id_type=MESH)
@@ -162,64 +163,51 @@
             visit(greet)
 
 
-        def remote(src, dst, ss, rs, dev):
+        def remote(src, dst, rs, dev):
             return pltpu.make_async_remote_copy(
-                src_ref=src, dst_ref=dst, send_sem=ss, recv_sem=rs, device_id=dev,
+                src_ref=src, dst_ref=dst, send_sem=sent, recv_sem=rs, device_id=dev,
                 device_id_type=MESH)
 
-        all_x = remote(xrecv, xrecv, xs, xr, xup)
-        all_y = remote(yrecv, yrecv, ys, yr, yup)
-        all_blends = remote(rbr, rbr, bs, br, xup)
-        others = mxr.at[0:total - 1]
-        all_tops = remote(others, others, ms, mr, xup)
-
-        pltpu.make_async_copy(u_in, st.at[0:5, BASE:BASE + rows], us).wait()
+        def all_of(ref, count, sem):
+            return remote(ref.at[0:count], ref.at[0:count], sem, xup)
+
+        pltpu.make_async_copy(u_in, st.at[0:5, BASE:BASE + rows], sent).wait()
         top = None
+        for r in range(0, rows, 8):
+            p = mechanics([st[f, BASE + r:BASE + r + 8, :] for f in range(5)])
+            speed = jnp.abs(p[0]) + jnp.abs(p[1]) + jnp.abs(p[2]) + 3.0 * p[4]
+            top = speed if top is None else jnp.maximum(top, speed)
+        mx[...] = jnp.max(top, axis=0, keepdims=True)
+        last = jnp.logical_and(wraps, ix >= ngx - 2)
+
+        def meet():
+            pl.semaphore_wait(barrier, jnp.where(root, 5, 6) + jnp.where(inner, 1, 0))
+
+            for (x, y), here in zip(roots, is_root):
+                @pl.when(jnp.logical_not(here))
+                def _():
+                    remote(mx, mxr.at[rank], tops, {"gx": x, "gy": y}).start()
+
+        pl.when(last)(meet)
+        lane = lax.broadcasted_iota(jnp.int32, (8, nz), 1)
+        k = lane % 4
+        k0, k1, k2, k3 = k == 0, k == 1, k == 2, k == 3
+
+        def lanes(values):
+            a, b, c, d = (float(v) for v in values)
+            return jnp.where(k0, a, jnp.where(k1, b, jnp.where(k2, c, d))).astype(jnp.float32)
+
+        def roll(x, s):
+            return pltpu.roll(x, s % nz, 1)
+
+        zcoef = {s: lanes([inverse[c, c + s] if 0 <= c + s < 4 else 0.0 for c in range(4)])
+                 for s in range(-3, 4)}
         for r in range(0, rows, 8):
             here = slice(BASE + r, BASE + r + 8)
             p = mechanics([st[f, here, :] for f in range(5)])
             for f in range(5):
                 st[VEL + f, here, :] = p[f]
-            speed = jnp.abs(p[0]) + jnp.abs(p[1]) + jnp.abs(p[2]) + 3.0 * p[4]
-            top = speed if top is None else jnp.maximum(top, speed)
-        mx[...] = jnp.max(top, axis=0, keepdims=True)
-        for f in range(5):
-            ysend[0, f] = st[f, pl.ds(BASE + ny - 1, nx, ny), :]
-            ysend[1, f] = st[f, pl.ds(BASE, nx, ny), :]
-        mxr[rank] = mx[...]
-
-        pl.semaphore_wait(barrier, jnp.where(root, 5, 6) + jnp.where(inner, 1, 0))
-
-        @pl.when(wraps)
-        def _():
-            pl.semaphore_signal(late, 1, device_id=yup, device_id_type=MESH)
-
-        for (x, y), here in zip(roots, is_root):
-            @pl.when(jnp.logical_not(here))
-            def _():
-                remote(mx, mxr.at[rank], ms, mr, {"gx": x, "gy": y}).start()
-
-        remote(ysend.at[0], yrecv.at[0], ys, yr, yup).start()
-        pl.when(inner)(lambda: remote(ysend.at[1], yrecv.at[1], ys, yr, ydn).start())
-        remote(st.at[0:5, BASE + rows - ny:BASE + rows], xrecv.at[0], xs, xr, xup).start()
-        remote(st.at[0:5, BASE:BASE + ny], xrecv.at[1], xs, xr, xdn).start()
-
-        lane = lax.broadcasted_iota(jnp.int32, (8, nz), 1)
-        k = lane % 4
-        k0, k1, k2, k3 = k == 0, k == 1, k == 2, k == 3
-
-        def lanes(values):
-            a, b, c, d = (float(v) for v in values)
-            return jnp.where(k0, a, jnp.where(k1, b, jnp.where(k2, c, d))).astype(jnp.float32)
-
-        def roll(x, s):
-            return pltpu.roll(x, s % nz, 1)
-
-        zcoef = {s: lanes([inverse[c, c + s] if 0 <= c + s < 4 else 0.0 for c in range(4)])
-                 for s in range(-3, 4)}
-        for r in range(0, rows, 8):
-            here = slice(BASE + r, BASE + r + 8)
-            q = st[0, here, :] * st[PRS, here, :]
+            q = st[0, here, :] * p[3]
             t = zcoef[0] * q
             for s in (-3, -2, -1, 1, 2, 3):
                 t = t + zcoef[s] * roll(q, -s)
@@ -257,10 +245,24 @@
             raw = 1.0 / (1.0 + jnp.exp(-sharp * (energy - threshold)))
             raw = jnp.minimum(raw, 0.5)
             rb[e] = raw
-        remote(rb, rbr.at[2], bs, br, yup).start()
-        pl.when(inner)(lambda: remote(rb, rbr.at[3], bs, br, ydn).start())
-        remote(rb, rbr.at[0], bs, br, xup).start()
-        remote(rb, rbr.at[1], bs, br, xdn).start()
+        for f in range(5):
+            ysend[0, f] = st[f, pl.ds(BASE + ny - 1, nx, ny), :]
+            ysend[1, f] = st[f, pl.ds(BASE, nx, ny), :]
+        mxr[rank] = mx[...]
+
+        pl.when(jnp.logical_not(last))(meet)
+        remote(ysend.at[0], yrecv.at[0], halo, yup).start()
+        pl.when(inner)(lambda: remote(ysend.at[1], yrecv.at[1], halo, ydn).start())
+        remote(st.at[0:5, BASE + rows - ny:BASE + rows], xrecv.at[0], halo, xup).start()
+        remote(st.at[0:5, BASE:BASE + ny], xrecv.at[1], halo, xdn).start()
+        remote(rb, rbr.at[2], halo, yup).start()
+        pl.when(inner)(lambda: remote(rb, rbr.at[3], halo, ydn).start())
+        remote(rb, rbr.at[0], halo, xup).start()
+        remote(rb, rbr.at[1], halo, xdn).start()
+
+        @pl.when(wraps)
+        def _():
+            pl.semaphore_signal(late, 1, device_id=yup, device_id_type=MESH)
 
         for r in range(0, rows, 8):
             here = slice(BASE + r, BASE + r + 8)
@@ -356,10 +358,10 @@
         @pl.when(jnp.logical_not(inner))
         def _():
             pl.semaphore_wait(late, 1)
-            remote(ysend.at[1], yrecv.at[1], ys, yr, ydn).start()
-            remote(rb, rbr.at[3], bs, br, ydn).start()
-
-        all_x.wait_recv()
+            remote(ysend.at[1], yrecv.at[1], halo, ydn).start()
+            remote(rb, rbr.at[3], halo, ydn).start()
+
+        all_of(span, parts, halo).wait_recv()
         for h in range(0, ny, 8):
             for side in range(2):
                 got = primitives([xrecv[side, f, h:h + 8, :] for f in range(5)])
@@ -371,8 +373,6 @@
                 for f in range(5):
                     vol[f, r:r + 8, :] += face[f] * scale
 
-        all_y.wait_recv()
-        all_blends.wait_recv()
         row = lax.broadcasted_iota(jnp.int32, (eyl, nz), 0)
         pick = (lax.broadcasted_iota(jnp.int32, (nz, nz // 4), 0)
                 == 4 * lax.broadcasted_iota(jnp.int32, (nz, nz // 4), 1)).astype(jnp.float32)
@@ -407,29 +407,25 @@
                     r = (4 * e + i) * ny + h
                     for f in range(5):
                         inc[f, r:r + 8, :] = vol[f, r:r + 8, :] + b * dif[f, r:r + 8, :]
-        for c in (all_x, all_y, all_blends):
-            c.wait_send()
-
-        for here in is_root:
-            @pl.when(jnp.logical_not(here))
+        for here, count in ((root, 2), (jnp.logical_not(root), 3)):
+            @pl.when(here)
             def _():
-                remote(mx, mxr.at[rank], ms, mr, xup).wait_send()
+                all_of(span, parts + count, tops).wait_send()
 
         @pl.when(root)
         def _():
-            all_tops.wait_recv()
-            tops = [mxr[i] for i in range(total)]
-            while len(tops) > 1:
-                pairs = [jnp.maximum(a, b) for a, b in zip(tops[::2], tops[1::2])]
-                tops = pairs + tops[2 * len(pairs):]
-            top_out[...] = tops[0]
+            all_of(mxr, total - 1, tops).wait_recv()
+            found = [mxr[i] for i in range(total)]
+            while len(found) > 1:
+                pairs = [jnp.maximum(a, b) for a, b in zip(found[::2], found[1::2])]
+                found = pairs + found[2 * len(pairs):]
 
             @pl.when(hub)
             def _():
-                mx2[...] = tops[0]
+                mx2[...] = found[0]
 
                 def spread(x, y):
-                    return remote(mx2, myr, ns, nr, {"gx": x, "gy": y})
+                    return remote(mx2, myr, tops, {"gx": x, "gy": y})
 
                 for y in range(min(ngy, 64 // ngx)):
                     for x in range(ngx):
@@ -440,17 +436,15 @@
                     spread(lax.rem(t, ngx), lax.div(t, ngx)).start()
                     return carry
 
-                def sent(t, carry):
-                    spread(0, 0).wait_send()
-                    return carry
-
                 if total > 64:
                     lax.fori_loop(64 // ngx * ngx, total, send, 0)
-                lax.fori_loop(0, total - len(roots), sent, 0)
+                all_of(mxr, total - len(roots), tops).wait_send()
+
+            top_out[...] = found[0]
 
         @pl.when(jnp.logical_not(root))
         def _():
-            remote(mx2, myr, ns, nr, xup).wait_recv()
+            remote(mx2, myr, tops, xup).wait_recv()
             top_out[...] = myr[...]
 
     f32 = jnp.float32
@@ -473,18 +467,24 @@
         pltpu.VMEM((1, nz), f32),
         pltpu.VMEM((total, 1, nz), f32),
         pltpu.VMEM((1, nz), f32),
-        dma, dma, dma, dma, dma, dma,
-        dma, dma, dma, dma, dma,
+        pltpu.VMEM((parts + 3, 1, nz), f32),
+        dma, dma, dma,
         pltpu.SemaphoreType.REGULAR,
     ]
     return kernel, scratch
 
 
-def finish(raw, smooth, top, inc, bl):
-    step = -0.25 / jnp.max(top[...], axis=(0, 1), keepdims=True)
+def finish(raw, smooth, top, inc, bl, scaled, done):
+    blend = pltpu.make_async_copy(smooth, bl, done)
+    blend.start()
+    peak = jnp.broadcast_to(top[...], (8, top.shape[1]))
+    step = -0.25 / jnp.max(peak, axis=1, keepdims=True)
     for f in range(5):
-        inc[f] = step * raw[f]
-    bl[...] = smooth[...]
+        for r in range(0, raw.shape[1], 8):
+            scaled[f, r:r + 8, :] = step * raw[f, r:r + 8, :]
+        pltpu.make_async_copy(scaled.at[f], inc.at[f], done).start()
+    pltpu.make_async_copy(scaled, inc, done).wait()
+    blend.wait()
 
 
 def solution(mesh):
@@ -510,7 +510,8 @@
             finish,
             out_shape=(shape(5, nx * ny, nz), shape(nx // 4, ny // 4, nz // 4)),
             in_specs=[vmem, vmem, vmem],
-            out_specs=(vmem, vmem),
+            out_specs=(pl.BlockSpec(memory_space=pltpu.HBM),) * 2,
+            scratch_shapes=[pltpu.VMEM((5, nx * ny, nz), jnp.float32), pltpu.SemaphoreType.DMA],
             compiler_params=pltpu.CompilerParams(vmem_limit_bytes=8 * 2**20),
             name="finish",
         )(raw, smooth, top)

time: 11.2 us -> 11 us (0.982)
  no operation moved by 1% of the time
where the time goes in v2:
time: 11 us; the launch traced here: 10.8 us
  Pallas kernels  10.2 us (93%)
  between operations  0.64 us (6%)
    pallas_call x1, Pallas kernels, body(): pl.pallas_call(kernel, out_shape=(shape(5, nx * ny, nz), shape(nx // 4, n...  9.44 us
    pallas_call x1, Pallas kernels, body(): pl.pallas_call(finish, out_shape=(shape(5, nx * ny, nz), shape(nx // 4, n...  0.75 us

profile of v2, /device:TPU:0, one launch (start us, length us, event | category | flops | bytes accessed | tf_op | source)
XLA Modules:
  0.0 10.8 jit_solution(3328488731314817898)
XLA Ops:
  0.6 9.4 %section.1 = (f32[5,64,128]{2,1,0:T(8,128)S(1)}, f32[1,4,32]{2,1,0:T(4,128)S(1)}, f32[1,128]{1,0:T(1,128)S(1)}) custom-call(f32[5,64,128]{2,1,0:T(8,128)} %bitcast.2), custom_call_target="tpu_custom_call" | custom-call | tf_op jit(solution)/shard_map/section/pallas_call | solution.py:498
  10.1 0.8 %finish.1 = (f32[5,64,128]{2,1,0:T(8,128)}, f32[1,4,32]{2,1,0:T(4,128)}) custom-call(f32[5,64,128]{2,1,0:T(8,128)S(1)} %get-tuple-element.7.raw, f32[1,4,32]{2,1,0:T(4,128)S(1)} %get-tuple-element.8.smooth, f32[1,128]{1,0:T(1,128)S(1)} %get-tuple-element.9.top), custom_call_target="tpu_custom_call" | custom-call | tf_op jit(solution)/shard_map/finish/pallas_call | solution.py:509

commit v3 on v2

--- a/solution.py
+++ b/solution.py
@@ -125,7 +125,7 @@
     exl, eyl, rows = nx // 4, ny // 4, nx * ny
     total = ngx * ngy
     parts = 10 * (nx + ny) + 4 * exl * eyl
-    roots = [(0, 0), (ngx - 1, 0), (1, 0)]
+    roots = [(0, 0), (ngx - 1, 0), (1, 1), (1, 0)]
     group = 8 if (nx * eyl) % 8 == 0 else 4
 
     def kernel(u_in, inc, smooth_out, top_out, st, vol, dif, tq, ysend, yrecv, xrecv, yown, rb, rbr, near,
@@ -137,8 +137,9 @@
         barrier = pltpu.get_barrier_semaphore()
         rank = iy * ngx + ix
         is_root = [rank == y * ngx + x for x, y in roots]
-        hub = is_root[1]
-        root = jnp.logical_or(jnp.logical_or(is_root[0], is_root[2]), hub)
+        root = is_root[0]
+        for here in is_root[1:]:
+            root = jnp.logical_or(root, here)
 
         def greet(device):
             pl.semaphore_signal(barrier, 1, device_id=device, device_id_type=MESH)
@@ -154,6 +155,7 @@
         xup, xdn = {"gx": lax.rem(ix + 1, ngx)}, {"gx": lax.rem(ix + ngx - 1, ngx)}
         yup, ydn = {"gy": lax.rem(iy + 1, ngy)}, {"gy": lax.rem(iy + ngy - 1, ngy)}
         inner, wraps = iy > 0, iy == ngy - 1
+        need = jnp.where(root, 6, 7) + jnp.where(inner, 1, 0)
         for device in (xup, xdn, ydn):
             greet(device)
         pl.when(jnp.logical_not(wraps))(lambda: greet(yup))
@@ -174,14 +176,18 @@
         pltpu.make_async_copy(u_in, st.at[0:5, BASE:BASE + rows], sent).wait()
         top = None
         for r in range(0, rows, 8):
-            p = mechanics([st[f, BASE + r:BASE + r + 8, :] for f in range(5)])
-            speed = jnp.abs(p[0]) + jnp.abs(p[1]) + jnp.abs(p[2]) + 3.0 * p[4]
+            density, m1, m2, m3, energy = [st[f, BASE + r:BASE + r + 8, :] for f in range(5)]
+            unit = 1.0 / density
+            v1, v2, v3 = m1 * unit, m2 * unit, m3 * unit
+            inside = energy - 0.5 * density * (v1 * v1 + v2 * v2 + v3 * v3)
+            sound = jnp.sqrt(gas_gamma * (gas_gamma - 1.0) * inside * unit)
+            speed = jnp.abs(v1) + jnp.abs(v2) + jnp.abs(v3) + 3.0 * sound
             top = speed if top is None else jnp.maximum(top, speed)
         mx[...] = jnp.max(top, axis=0, keepdims=True)
         last = jnp.logical_and(wraps, ix >= ngx - 2)
 
         def meet():
-            pl.semaphore_wait(barrier, jnp.where(root, 5, 6) + jnp.where(inner, 1, 0))
+            pl.semaphore_wait(barrier, need)
 
             for (x, y), here in zip(roots, is_root):
                 @pl.when(jnp.logical_not(here))
@@ -407,7 +413,7 @@
                     r = (4 * e + i) * ny + h
                     for f in range(5):
                         inc[f, r:r + 8, :] = vol[f, r:r + 8, :] + b * dif[f, r:r + 8, :]
-        for here, count in ((root, 2), (jnp.logical_not(root), 3)):
+        for here, count in ((root, 3), (jnp.logical_not(root), 4)):
             @pl.when(here)
             def _():
                 all_of(span, parts + count, tops).wait_send()
@@ -420,25 +426,25 @@
                 pairs = [jnp.maximum(a, b) for a, b in zip(found[::2], found[1::2])]
                 found = pairs + found[2 * len(pairs):]
 
-            @pl.when(hub)
-            def _():
-                mx2[...] = found[0]
-
-                def spread(x, y):
-                    return remote(mx2, myr, tops, {"gx": x, "gy": y})
-
-                for y in range(min(ngy, 64 // ngx)):
-                    for x in range(ngx):
-                        if (x, y) not in roots:
-                            spread(x, y).start()
-
-                def send(t, carry):
-                    spread(lax.rem(t, ngx), lax.div(t, ngx)).start()
-                    return carry
-
-                if total > 64:
-                    lax.fori_loop(64 // ngx * ngx, total, send, 0)
-                all_of(mxr, total - len(roots), tops).wait_send()
+            for hub, mine in ((1, lambda x, odd: x >= 2 or not odd), (2, lambda x, odd: x < 2 and odd)):
+                @pl.when(is_root[hub])
+                def _():
+                    mx2[...] = found[0]
+
+                    def send(h, carry):
+                        for odd in range(2):
+                            for x in range(ngx):
+                                if mine(x, odd) and not (isinstance(h, int) and (x, 2 * h + odd) in roots):
+                                    remote(mx2, myr, tops, {"gx": x, "gy": 2 * h + odd}).start()
+                        return carry
+
+                    for h in range(min(ngy // 2, 16)):
+                        send(h, 0)
+                    if ngy > 32:
+                        lax.fori_loop(16, ngy // 2, send, 0)
+                    count = sum(mine(x, y % 2) and (x, y) not in roots
+                                for x in range(ngx) for y in range(ngy))
+                    all_of(mxr, count, tops).wait_send()
 
             top_out[...] = found[0]
 
@@ -467,7 +473,7 @@
         pltpu.VMEM((1, nz), f32),
         pltpu.VMEM((total, 1, nz), f32),
         pltpu.VMEM((1, nz), f32),
-        pltpu.VMEM((parts + 3, 1, nz), f32),
+        pltpu.VMEM((parts + 4, 1, nz), f32),
         dma, dma, dma,
         pltpu.SemaphoreType.REGULAR,
     ]

time: 11 us -> 11 us (level)
  no operation moved by 1% of the time
where the time goes in v3:
time: 11 us; the launch traced here: 10.8 us
  Pallas kernels  10.2 us (93%)
  between operations  0.64 us (6%)
    pallas_call x1, Pallas kernels, body(): pl.pallas_call(kernel, out_shape=(shape(5, nx * ny, nz), shape(nx // 4, n...  9.44 us
    pallas_call x1, Pallas kernels, body(): pl.pallas_call(finish, out_shape=(shape(5, nx * ny, nz), shape(nx // 4, n...  0.75 us

profile of v3, /device:TPU:0, one launch (start us, length us, event | category | flops | bytes accessed | tf_op | source)
XLA Modules:
  0.0 10.8 jit_solution(12750562329216473356)
XLA Ops:
  0.6 9.4 %section.1 = (f32[5,64,128]{2,1,0:T(8,128)S(1)}, f32[1,4,32]{2,1,0:T(4,128)S(1)}, f32[1,128]{1,0:T(1,128)S(1)}) custom-call(f32[5,64,128]{2,1,0:T(8,128)} %bitcast.2), custom_call_target="tpu_custom_call" | custom-call | tf_op jit(solution)/shard_map/section/pallas_call | solution.py:504
  10.1 0.8 %finish.1 = (f32[5,64,128]{2,1,0:T(8,128)}, f32[1,4,32]{2,1,0:T(4,128)}) custom-call(f32[5,64,128]{2,1,0:T(8,128)S(1)} %get-tuple-element.7.raw, f32[1,4,32]{2,1,0:T(4,128)S(1)} %get-tuple-element.8.smooth, f32[1,128]{1,0:T(1,128)S(1)} %get-tuple-element.9.top), custom_call_target="tpu_custom_call" | custom-call | tf_op jit(solution)/shard_map/finish/pallas_call | solution.py:515

commit v4 on v3

--- a/solution.py
+++ b/solution.py
@@ -418,40 +418,43 @@
             def _():
                 all_of(span, parts + count, tops).wait_send()
 
-        @pl.when(root)
-        def _():
+        def gather():
             all_of(mxr, total - 1, tops).wait_recv()
             found = [mxr[i] for i in range(total)]
             while len(found) > 1:
                 pairs = [jnp.maximum(a, b) for a, b in zip(found[::2], found[1::2])]
                 found = pairs + found[2 * len(pairs):]
-
-            for hub, mine in ((1, lambda x, odd: x >= 2 or not odd), (2, lambda x, odd: x < 2 and odd)):
-                @pl.when(is_root[hub])
-                def _():
-                    mx2[...] = found[0]
-
-                    def send(h, carry):
-                        for odd in range(2):
-                            for x in range(ngx):
-                                if mine(x, odd) and not (isinstance(h, int) and (x, 2 * h + odd) in roots):
-                                    remote(mx2, myr, tops, {"gx": x, "gy": 2 * h + odd}).start()
-                        return carry
-
-                    for h in range(min(ngy // 2, 16)):
-                        send(h, 0)
-                    if ngy > 32:
-                        lax.fori_loop(16, ngy // 2, send, 0)
-                    count = sum(mine(x, y % 2) and (x, y) not in roots
-                                for x in range(ngx) for y in range(ngy))
-                    all_of(mxr, count, tops).wait_send()
-
-            top_out[...] = found[0]
+            return found[0]
+
+        for hub, mine in ((1, lambda x, odd: x >= 2 or not odd), (2, lambda x, odd: x < 2 and odd)):
+            @pl.when(is_root[hub])
+            def _():
+                mx2[...] = gather()
+
+                def send(h, carry):
+                    for odd in range(2):
+                        for x in range(ngx):
+                            if mine(x, odd) and not (isinstance(h, int) and (x, 2 * h + odd) in roots):
+                                remote(mx2, myr, tops, {"gx": x, "gy": 2 * h + odd}).start()
+                    return carry
+
+                for h in range(min(ngy // 2, 16)):
+                    send(h, 0)
+                if ngy > 32:
+                    lax.fori_loop(16, ngy // 2, send, 0)
+                top_out[...] = mx2[...]
+                count = sum(mine(x, y % 2) and (x, y) not in roots
+                            for x in range(ngx) for y in range(ngy))
+                all_of(mxr, count, tops).wait_send()
 
         @pl.when(jnp.logical_not(root))
         def _():
             remote(mx2, myr, tops, xup).wait_recv()
             top_out[...] = myr[...]
+
+        @pl.when(jnp.logical_or(is_root[0], is_root[3]))
+        def _():
+            top_out[...] = gather()
 
     f32 = jnp.float32
     dma = pltpu.SemaphoreType.DMA

time: 11 us -> 11 us (level)
  no operation moved by 1% of the time
where the time goes in v4:
time: 11 us; the launch traced here: 10.8 us
  Pallas kernels  10.2 us (93%)
  between operations  0.64 us (6%)
    pallas_call x1, Pallas kernels, body(): pl.pallas_call(kernel, out_shape=(shape(5, nx * ny, nz), shape(nx // 4, n...  9.44 us
    pallas_call x1, Pallas kernels, body(): pl.pallas_call(finish, out_shape=(shape(5, nx * ny, nz), shape(nx // 4, n...  0.75 us

profile of v4, /device:TPU:0, one launch (start us, length us, event | category | flops | bytes accessed | tf_op | source)
XLA Modules:
  0.0 10.8 jit_solution(15953902134232140230)
XLA Ops:
  0.6 9.4 %section.1 = (f32[5,64,128]{2,1,0:T(8,128)S(1)}, f32[1,4,32]{2,1,0:T(4,128)S(1)}, f32[1,128]{1,0:T(1,128)S(1)}) custom-call(f32[5,64,128]{2,1,0:T(8,128)} %bitcast.2), custom_call_target="tpu_custom_call" | custom-call | tf_op jit(solution)/shard_map/section/pallas_call | solution.py:507
  10.1 0.8 %finish.1 = (f32[5,64,128]{2,1,0:T(8,128)}, f32[1,4,32]{2,1,0:T(4,128)}) custom-call(f32[5,64,128]{2,1,0:T(8,128)S(1)} %get-tuple-element.7.raw, f32[1,4,32]{2,1,0:T(4,128)S(1)} %get-tuple-element.8.smooth, f32[1,128]{1,0:T(1,128)S(1)} %get-tuple-element.9.top), custom_call_target="tpu_custom_call" | custom-call | tf_op jit(solution)/shard_map/finish/pallas_call | solution.py:518

commit v5 on v4

--- a/solution.py
+++ b/solution.py
@@ -488,10 +488,14 @@
     blend.start()
     peak = jnp.broadcast_to(top[...], (8, top.shape[1]))
     step = -0.25 / jnp.max(peak, axis=1, keepdims=True)
+    rows = raw.shape[1]
+    half = max(rows // 16 * 8, 8)
     for f in range(5):
-        for r in range(0, raw.shape[1], 8):
-            scaled[f, r:r + 8, :] = step * raw[f, r:r + 8, :]
-        pltpu.make_async_copy(scaled.at[f], inc.at[f], done).start()
+        for low in range(0, rows, half):
+            high = min(low + half, rows)
+            for r in range(low, high, 8):
+                scaled[f, r:r + 8, :] = step * raw[f, r:r + 8, :]
+            pltpu.make_async_copy(scaled.at[f, low:high], inc.at[f, low:high], done).start()
     pltpu.make_async_copy(scaled, inc, done).wait()
     blend.wait()
 

time: 11 us -> 11 us (level)
  no operation moved by 1% of the time
where the time goes in v5:
time: 11 us; the launch traced here: 10.8 us
  Pallas kernels  10.2 us (93%)
  between operations  0.64 us (6%)
    pallas_call x1, Pallas kernels, body(): pl.pallas_call(kernel, out_shape=(shape(5, nx * ny, nz), shape(nx // 4, n...  9.44 us
    pallas_call x1, Pallas kernels, body(): pl.pallas_call(finish, out_shape=(shape(5, nx * ny, nz), shape(nx // 4, n...  0.75 us

profile of v5, /device:TPU:0, one launch (start us, length us, event | category | flops | bytes accessed | tf_op | source)
XLA Modules:
  0.0 10.8 jit_solution(2494726796822300304)
XLA Ops:
  0.6 9.4 %section.1 = (f32[5,64,128]{2,1,0:T(8,128)S(1)}, f32[1,4,32]{2,1,0:T(4,128)S(1)}, f32[1,128]{1,0:T(1,128)S(1)}) custom-call(f32[5,64,128]{2,1,0:T(8,128)} %bitcast.2), custom_call_target="tpu_custom_call" | custom-call | tf_op jit(solution)/shard_map/section/pallas_call | solution.py:511
  10.1 0.7 %finish.1 = (f32[5,64,128]{2,1,0:T(8,128)}, f32[1,4,32]{2,1,0:T(4,128)}) custom-call(f32[5,64,128]{2,1,0:T(8,128)S(1)} %get-tuple-element.7.raw, f32[1,4,32]{2,1,0:T(4,128)S(1)} %get-tuple-element.8.smooth, f32[1,128]{1,0:T(1,128)S(1)} %get-tuple-element.9.top), custom_call_target="tpu_custom_call" | custom-call | tf_op jit(solution)/shard_map/finish/pallas_call | solution.py:522

commit v6 on v5

--- a/solution.py
+++ b/solution.py
@@ -298,7 +298,7 @@
         mr_ = lanes([2 * deriv[0, 3], 0.0, 2 * deriv[2, 0], 2 * deriv[3, 1]])
 
         def z_group(g, carry):
-            row = g * 8
+            row = pl.multiple_of(g * 8, 8)
             own = [st[f, pl.ds(row + BASE, 8), :] for f in range(FIELDS)]
             nxt = [roll(x, -1) for x in own]
             far = [None] * FIELDS
@@ -315,8 +315,7 @@
                     (da * g1[f] - cam * f1[f]) + roll(db * g1[f] - cbm * f1[f], 1) - mm)
             return carry
 
-        for g in range(rows // 8):
-            z_group(g, 0)
+        lax.fori_loop(0, rows // 8, z_group, 0)
 
         for e in range(exl):
             for h in range(0, ny, 8):

time: 11 us -> 11 us (level)
  no operation moved by 1% of the time
where the time goes in v6:
time: 11 us; the launch traced here: 10.8 us
  Pallas kernels  10.2 us (93%)
  between operations  0.64 us (6%)
    pallas_call x1, Pallas kernels, body(): pl.pallas_call(kernel, out_shape=(shape(5, nx * ny, nz), shape(nx // 4, n...  9.44 us
    pallas_call x1, Pallas kernels, body(): pl.pallas_call(finish, out_shape=(shape(5, nx * ny, nz), shape(nx // 4, n...  0.75 us

profile of v6, /device:TPU:0, one launch (start us, length us, event | category | flops | bytes accessed | tf_op | source)
XLA Modules:
  0.0 10.8 jit_solution(15996502715435627572)
XLA Ops:
  0.6 9.4 %section.1 = (f32[5,64,128]{2,1,0:T(8,128)S(1)}, f32[1,4,32]{2,1,0:T(4,128)S(1)}, f32[1,128]{1,0:T(1,128)S(1)}) custom-call(f32[5,64,128]{2,1,0:T(8,128)} %bitcast.2), custom_call_target="tpu_custom_call" | custom-call | tf_op jit(solution)/shard_map/section/pallas_call | solution.py:510
  10.1 0.7 %finish.1 = (f32[5,64,128]{2,1,0:T(8,128)}, f32[1,4,32]{2,1,0:T(4,128)}) custom-call(f32[5,64,128]{2,1,0:T(8,128)S(1)} %get-tuple-element.7.raw, f32[1,4,32]{2,1,0:T(4,128)S(1)} %get-tuple-element.8.smooth, f32[1,128]{1,0:T(1,128)S(1)} %get-tuple-element.9.top), custom_call_target="tpu_custom_call" | custom-call | tf_op jit(solution)/shard_map/finish/pallas_call | solution.py:521

commit v7 on v6

--- a/solution.py
+++ b/solution.py
@@ -192,7 +192,7 @@
             for (x, y), here in zip(roots, is_root):
                 @pl.when(jnp.logical_not(here))
                 def _():
-                    remote(mx, mxr.at[rank], tops, {"gx": x, "gy": y}).start()
+                    remote(mx, mxr.at[pl.ds(rank, 1)], tops, {"gx": x, "gy": y}).start()
 
         pl.when(last)(meet)
         lane = lax.broadcasted_iota(jnp.int32, (8, nz), 1)
@@ -254,7 +254,7 @@
         for f in range(5):
             ysend[0, f] = st[f, pl.ds(BASE + ny - 1, nx, ny), :]
             ysend[1, f] = st[f, pl.ds(BASE, nx, ny), :]
-        mxr[rank] = mx[...]
+        mxr[pl.ds(rank, 1), :] = mx[...]
 
         pl.when(jnp.logical_not(last))(meet)
         remote(ysend.at[0], yrecv.at[0], halo, yup).start()
@@ -418,12 +418,12 @@
                 all_of(span, parts + count, tops).wait_send()
 
         def gather():
-            all_of(mxr, total - 1, tops).wait_recv()
-            found = [mxr[i] for i in range(total)]
+            all_of(span, total - 1, tops).wait_recv()
+            found = [mxr[i:i + 8, :] for i in range(0, total, 8)]
             while len(found) > 1:
                 pairs = [jnp.maximum(a, b) for a, b in zip(found[::2], found[1::2])]
                 found = pairs + found[2 * len(pairs):]
-            return found[0]
+            return jnp.max(found[0], axis=0, keepdims=True)
 
         for hub, mine in ((1, lambda x, odd: x >= 2 or not odd), (2, lambda x, odd: x < 2 and odd)):
             @pl.when(is_root[hub])
@@ -444,7 +444,7 @@
                 top_out[...] = mx2[...]
                 count = sum(mine(x, y % 2) and (x, y) not in roots
                             for x in range(ngx) for y in range(ngy))
-                all_of(mxr, count, tops).wait_send()
+                all_of(span, count, tops).wait_send()
 
         @pl.when(jnp.logical_not(root))
         def _():
@@ -473,9 +473,9 @@
         pltpu.VMEM((exl, eyl, nz), f32),
         pltpu.VMEM((1, nz), f32),
         pltpu.VMEM((1, nz), f32),
-        pltpu.VMEM((total, 1, nz), f32),
+        pltpu.VMEM((total, nz), f32),
         pltpu.VMEM((1, nz), f32),
-        pltpu.VMEM((parts + 4, 1, nz), f32),
+        pltpu.VMEM((max(parts + 4, total), 1, nz), f32),
         dma, dma, dma,
         pltpu.SemaphoreType.REGULAR,
     ]

time: 11 us -> 11 us (level)
  no operation moved by 1% of the time
where the time goes in v7:
time: 11 us; the launch traced here: 10.8 us
  Pallas kernels  10.2 us (93%)
  between operations  0.64 us (6%)
    pallas_call x1, Pallas kernels, body(): pl.pallas_call(kernel, out_shape=(shape(5, nx * ny, nz), shape(nx // 4, n...  9.44 us
    pallas_call x1, Pallas kernels, body(): pl.pallas_call(finish, out_shape=(shape(5, nx * ny, nz), shape(nx // 4, n...  0.75 us

profile of v7, /device:TPU:0, one launch (start us, length us, event | category | flops | bytes accessed | tf_op | source)
XLA Modules:
  0.0 10.8 jit_solution(1230717479303066577)
XLA Ops:
  0.6 9.4 %section.1 = (f32[5,64,128]{2,1,0:T(8,128)S(1)}, f32[1,4,32]{2,1,0:T(4,128)S(1)}, f32[1,128]{1,0:T(1,128)S(1)}) custom-call(f32[5,64,128]{2,1,0:T(8,128)} %bitcast.2), custom_call_target="tpu_custom_call" | custom-call | tf_op jit(solution)/shard_map/section/pallas_call | solution.py:510
  10.1 0.7 %finish.1 = (f32[5,64,128]{2,1,0:T(8,128)}, f32[1,4,32]{2,1,0:T(4,128)}) custom-call(f32[5,64,128]{2,1,0:T(8,128)S(1)} %get-tuple-element.7.raw, f32[1,4,32]{2,1,0:T(4,128)S(1)} %get-tuple-element.8.smooth, f32[1,128]{1,0:T(1,128)S(1)} %get-tuple-element.9.top), custom_call_target="tpu_custom_call" | custom-call | tf_op jit(solution)/shard_map/finish/pallas_call | solution.py:521
